TPU v7x, 32 devices: a whole 2x2x4 slice. The times are simulated.
32 devices in a mesh: shard: 2 (over core), ctx: 4 (over y, x), tp: 4 (over z).
Axes of the slice: x: 2, y: 2, z: 4, core: 2. Of those that a mesh axis runs over, the one named last changes fastest.
Arguments:
- layer_input: bfloat16 [8, 1024, 2048], P('shard', 'ctx'), may hold values from -6 to 6
- output_gradient: bfloat16 [8, 1024, 2048], P('shard', 'ctx'), may hold values from -6 to 6
- picture_piece_starts: int32 [8, 2], P('shard'), may hold values from 0 to 768, as said below
- sequence_adapter_index: int32 [8], P('shard'), may hold values from 0 to 7
- attention_norm_gain: float32 [2048], replicated, may hold values from 0.5 to 1.5
- attention_norm_bias: float32 [2048], replicated, may hold values from -1 to 1
- feedforward_norm_gain: float32 [2048], replicated, may hold values from 0.5 to 1.5
- feedforward_norm_bias: float32 [2048], replicated, may hold values from -1 to 1
- query_key_value_weight: bfloat16 [2048, 3, 2048], P('shard', None, 'tp'), may hold values from -0.125 to 0.125
- attention_output_weight: bfloat16 [2048, 2048], P('tp', 'shard'), may hold values from -0.375 to 0.375
- up_projection_weight: bfloat16 [2048, 8192], P('shard', 'tp'), may hold values from -0.125 to 0.125
- down_projection_weight: bfloat16 [8192, 2048], P('tp', 'shard'), may hold values from -0.09375 to 0.09375
- adapter_projection_first: bfloat16 [8, 2048, 16], replicated, may hold values from -0.125 to 0.125
- adapter_projection_second: bfloat16 [8, 16, 3, 2048], P(None, None, None, 'tp'), may hold values from -0.75 to 0.75
- adapter_heads_first: bfloat16 [8, 2048, 16], P(None, 'tp'), may hold values from -0.375 to 0.375
- adapter_heads_second: bfloat16 [8, 16, 2048], replicated, may hold values from -0.75 to 0.75
- adapter_up_first: bfloat16 [8, 2048, 16], replicated, may hold values from -0.125 to 0.125
- adapter_up_second: bfloat16 [8, 16, 8192], P(None, None, 'tp'), may hold values from -0.75 to 0.75
- adapter_down_first: bfloat16 [8, 8192, 16], P(None, 'tp'), may hold values from -0.09375 to 0.09375
- adapter_down_second: bfloat16 [8, 16, 2048], replicated, may hold values from -0.75 to 0.75
Outputs:
- layer_out: bfloat16 [8, 1024, 2048], P('shard', 'ctx')
- input_grad: bfloat16 [8, 1024, 2048], P('shard', 'ctx')
- qkv_in_grad: float32 [8, 2048, 16], replicated
- qkv_out_grad: float32 [8, 16, 3, 2048], P(None, None, None, 'tp')
- heads_in_grad: float32 [8, 2048, 16], P(None, 'tp')
- heads_out_grad: float32 [8, 16, 2048], replicated
- up_in_grad: float32 [8, 2048, 16], replicated
- up_out_grad: float32 [8, 16, 8192], P(None, None, 'tp')
- down_in_grad: float32 [8, 8192, 16], P(None, 'tp')
- down_out_grad: float32 [8, 16, 2048], replicated
Inputs may be any that keep to these rules, and one draw needn't show every extreme that they name: `picture_piece_starts`: piece c of a sequence starts within positions c * 512 to (c + 1) * 512 - 256, so pieces never meet; in some sequence a piece starts at 0, in some sequence a piece ends at 1024.
All inputs are finite; a program needn't handle non-finite values.
Results may differ from a plain program's by a relative error of at most 0.019.
Values may be sent and summed in bfloat16 or wider, within the bound.
A program may use at most 320 MiB of HBM per device.

v0:
```python
import jax
import jax.numpy as jnp
from jax import lax
from jax.sharding import PartitionSpec as P

HD = 128
PIC = 256
NORM_EPS = 1e-05


def layer_norm(inputs, gains, biases):
    average = jnp.mean(inputs, axis=-1, keepdims=True)
    centred = inputs - average
    spread = jnp.mean(centred * centred, axis=-1, keepdims=True)
    return centred * lax.rsqrt(spread + NORM_EPS) * gains + biases


def gelu_tanh(inputs):
    return (
        0.5
        * inputs
        * (1.0 + jnp.tanh(0.7978845608028654 * (inputs + 0.044715 * inputs * inputs * inputs)))
    )


def flattened_first(adapter_mat):
    adapter_tables, inner_dim, rank_width = adapter_mat.shape
    return jnp.transpose(adapter_mat, (1, 0, 2)).reshape(inner_dim, adapter_tables * rank_width)


def flattened_second(adapter_mat):
    return adapter_mat.reshape(adapter_mat.shape[0] * adapter_mat.shape[1], -1)


def unflat_in(grad_flat, adapter_tables):
    inner_dim = grad_flat.shape[0]
    return jnp.transpose(grad_flat.reshape(inner_dim, adapter_tables, -1), (1, 0, 2))


def matmul(left_mat, right_mat):
    return jnp.dot(left_mat, right_mat, preferred_element_type=jnp.float32)


def matmul_tn(left_mat, right_mat):
    return lax.dot_general(
        left_mat, right_mat, (((0,), (0,)), ((), ())), preferred_element_type=jnp.float32
    )


def matmul_nt(left_mat, right_mat):
    return lax.dot_general(
        left_mat, right_mat, (((1,), (1,)), ((), ())), preferred_element_type=jnp.float32
    )


def piece_labels(starts, positions):
    inside = (positions[None, None, :] >= starts[:, :, None]) & (
        positions[None, None, :] < starts[:, :, None] + PIC
    )
    labels = jnp.arange(1, starts.shape[1] + 1, dtype=jnp.int32)
    return jnp.sum(jnp.where(inside, labels[None, :, None], 0), axis=1)


def visible(query_pos, key_pos, query_labels, key_labels):
    causal = key_pos[None, None, :] <= query_pos[None, :, None]
    shared = (query_labels[:, :, None] == key_labels[:, None, :]) & (query_labels[:, :, None] > 0)
    return causal | shared


def exponents(queries, key_rows, query_pos, key_pos, visible_mask, slopes):
    score_scale = queries.shape[-1] ** (-0.5)
    logits = (
        jnp.einsum("sqhd,skhd->shqk", queries, key_rows, preferred_element_type=jnp.float32)
        * score_scale
    )
    distance = jnp.abs(query_pos[:, None] - key_pos[None, :]).astype(jnp.float32)
    logits = logits - slopes[None, :, None, None] * distance[None, None]
    return jnp.where(visible_mask[:, None], jnp.exp(logits), 0.0)


def block_grads(
    queries, scaled_grad, row_delta, key_rows, value_rows, query_pos, key_pos, visible_mask, slopes
):
    score_scale = queries.shape[-1] ** (-0.5)
    exponent = exponents(queries, key_rows, query_pos, key_pos, visible_mask, slopes)
    products_gv = jnp.einsum(
        "sqhd,skhd->shqk", scaled_grad, value_rows, preferred_element_type=jnp.float32
    )
    grad_logits = (
        exponent * (products_gv - jnp.transpose(row_delta, (0, 2, 1))[..., None])
    ).astype(jnp.bfloat16)
    grad_queries = (
        jnp.einsum("shqk,skhd->sqhd", grad_logits, key_rows, preferred_element_type=jnp.float32)
        * score_scale
    )
    grad_keyrows = (
        jnp.einsum("shqk,sqhd->skhd", grad_logits, queries, preferred_element_type=jnp.float32)
        * score_scale
    )
    grad_valrows = jnp.einsum(
        "shqk,sqhd->skhd",
        exponent.astype(jnp.bfloat16),
        scaled_grad,
        preferred_element_type=jnp.float32,
    )
    return (grad_queries, grad_keyrows, grad_valrows)


def tp_rows(rows_array, tp_count):
    chunk = rows_array.shape[0] // tp_count
    return lax.dynamic_slice_in_dim(rows_array, lax.axis_index("tp") * chunk, chunk, axis=0)


def scatter_rows(partials):
    widths = [part.shape[1] for part in partials]
    joined = lax.psum_scatter(
        jnp.concatenate(partials, axis=1), "tp", scatter_dimension=0, tiled=True
    )
    return split_columns(joined, widths)


def gather_rows(rows_here):
    widths = [part.shape[1] for part in rows_here]
    joined = lax.all_gather(jnp.concatenate(rows_here, axis=1), "tp", axis=0, tiled=True)
    return split_columns(joined, widths)


def split_columns(joined, widths):
    parts, offset = ([], 0)
    for width in widths:
        parts.append(joined[:, offset : offset + width])
        offset += width
    return tuple(parts)


def body(
    layer_input,
    output_gradient,
    picture_piece_starts,
    sequence_adapter_index,
    attention_norm_gain,
    attention_norm_bias,
    feedforward_norm_gain,
    feedforward_norm_bias,
    query_key_value_weight,
    attention_output_weight,
    up_projection_weight,
    down_projection_weight,
    adapter_projection_first,
    adapter_projection_second,
    adapter_heads_first,
    adapter_heads_second,
    adapter_up_first,
    adapter_up_second,
    adapter_down_first,
    adapter_down_second,
):
    seq_here, local_len, model_width = layer_input.shape
    tok_rows = seq_here * local_len
    tp_count = lax.axis_size("tp")
    adapter_tables = adapter_projection_first.shape[0]
    rank_width = adapter_projection_first.shape[2]
    head_width = HD
    device_heads = adapter_projection_second.shape[-1] // head_width
    local_width = device_heads * head_width
    columns = jnp.arange(adapter_tables * rank_width, dtype=jnp.int32) // rank_width
    chosen = (sequence_adapter_index[:, None] == columns[None, :]).astype(jnp.float32)
    select = jnp.broadcast_to(
        chosen[:, None, :], (seq_here, local_len, adapter_tables * rank_width)
    ).reshape(tok_rows, adapter_tables * rank_width)
    select_here = tp_rows(select, tp_count)
    head_ids = lax.axis_index("tp") * device_heads + jnp.arange(device_heads, dtype=jnp.int32)
    slopes = jnp.exp2(-8.0 * (head_ids.astype(jnp.float32) + 1.0) / (device_heads * tp_count))
    here_pos = lax.axis_index("ctx") * local_len + jnp.arange(local_len, dtype=jnp.int32)
    here_labels = piece_labels(picture_piece_starts, here_pos)
    heads_full = lax.all_gather(
        lax.all_gather(attention_output_weight, "tp", axis=0, tiled=True),
        "shard",
        axis=1,
        tiled=True,
    )
    heads_first_all = lax.all_gather(adapter_heads_first, "tp", axis=1, tiled=True)
    projection_first_flattened = flattened_first(adapter_projection_first)
    projection_second_flattened = flattened_second(adapter_projection_second)
    heads_first_flattened = flattened_first(adapter_heads_first)
    heads_first_all_flattened = flattened_first(heads_first_all)
    heads_second_flattened = flattened_second(adapter_heads_second)
    up_first_flattened = flattened_first(adapter_up_first)
    up_second_flattened = flattened_second(adapter_up_second)
    down_first_flattened = flattened_first(adapter_down_first)
    down_second_flattened = flattened_second(adapter_down_second)
    residual = layer_input.reshape(tok_rows, model_width).astype(jnp.float32)
    residual_here = tp_rows(residual, tp_count)
    first_norm = layer_norm(residual, attention_norm_gain, attention_norm_bias)
    first_act = first_norm.astype(jnp.bfloat16)
    _, first_back_full = jax.vjp(
        lambda inputs: layer_norm(inputs, attention_norm_gain, attention_norm_bias), residual_here
    )
    gathered_rows = (
        lax.all_gather(query_key_value_weight, "shard", axis=0, tiled=True),
        lax.all_gather(up_projection_weight, "shard", axis=0, tiled=True),
    )
    qkv_full = gathered_rows[0].reshape(model_width, 3 * local_width)
    up_full = gathered_rows[1]
    down_full = lax.all_gather(down_projection_weight, "shard", axis=1, tiled=True)
    first_low = (matmul(first_act, projection_first_flattened) * select).astype(jnp.bfloat16)
    projected = (
        matmul(first_act, qkv_full) + matmul(first_low, projection_second_flattened)
    ).astype(jnp.bfloat16)
    queries_flat = projected[:, :local_width].reshape(seq_here, local_len, local_width)
    queries = queries_flat.reshape(seq_here, local_len, device_heads, head_width)
    key_rows = projected[:, local_width : 2 * local_width].reshape(seq_here, local_len, local_width)
    value_rows = projected[:, 2 * local_width :].reshape(seq_here, local_len, local_width)
    pieces = (
        lax.all_gather(key_rows, "ctx", axis=1, tiled=True),
        lax.all_gather(value_rows, "ctx", axis=1, tiled=True),
    )
    piece_len = pieces[0].shape[1]
    key_pos = jnp.arange(piece_len, dtype=jnp.int32)
    key_labels = piece_labels(picture_piece_starts, key_pos)
    visible_mask = visible(here_pos, key_pos, here_labels, key_labels)
    piece_keys = pieces[0].reshape(seq_here, piece_len, device_heads, head_width)
    piece_values = pieces[1].reshape(seq_here, piece_len, device_heads, head_width)
    exponent = exponents(queries, piece_keys, here_pos, key_pos, visible_mask, slopes)
    weighted = jnp.einsum(
        "shqk,skhd->sqhd",
        exponent.astype(jnp.bfloat16),
        piece_values,
        preferred_element_type=jnp.float32,
    )
    weighted, totals = (weighted, jnp.sum(exponent, axis=-1))
    per_total = jnp.transpose(totals, (0, 2, 1))[..., None]
    heads_raw = weighted / per_total
    heads_act = heads_raw.reshape(tok_rows, local_width).astype(jnp.bfloat16)
    heads_act_here = lax.all_to_all(heads_act, "tp", 0, 1, tiled=True)
    attn_here = matmul(heads_act_here, heads_full)
    heads_low_here = (matmul(heads_act_here, heads_first_all_flattened) * select_here).astype(
        jnp.bfloat16
    )
    middle_here = residual_here + attn_here + matmul(heads_low_here, heads_second_flattened)
    second_norm, second_back = jax.vjp(
        lambda inputs: layer_norm(inputs, feedforward_norm_gain, feedforward_norm_bias), middle_here
    )
    second_act_here = second_norm.astype(jnp.bfloat16)
    (second_act,) = gather_rows((second_act_here,))
    up_low = (matmul(second_act, up_first_flattened) * select).astype(jnp.bfloat16)
    hidden = matmul(second_act, up_full) + matmul(up_low, up_second_flattened)
    activated, gelu_back = jax.vjp(gelu_tanh, hidden)
    activated = activated.astype(jnp.bfloat16)
    down_part = matmul(activated, down_full)
    down_low_part = matmul(activated, down_first_flattened)
    ffn_here, ffn_low_here = scatter_rows((down_part, down_low_part))
    down_low_here = (ffn_low_here * select_here).astype(jnp.bfloat16)
    result_here = (middle_here + ffn_here + matmul(down_low_here, down_second_flattened)).astype(
        jnp.bfloat16
    )
    result_rows, down_low = gather_rows((result_here, down_low_here))
    layer_out = result_rows.reshape(layer_input.shape)
    grad_top_low = output_gradient.reshape(tok_rows, model_width)
    grad_top_here = tp_rows(grad_top_low, tp_count).astype(jnp.float32)
    down_back = (matmul_nt(grad_top_low, down_second_flattened) * select).astype(jnp.bfloat16)
    grad_down_in = matmul_tn(activated, down_back)
    grad_activated = matmul_nt(grad_top_low, down_full) + matmul_nt(down_back, down_first_flattened)
    grad_hidden = gelu_back(grad_activated)[0].astype(jnp.bfloat16)
    up_second_gradient = matmul_tn(up_low, grad_hidden)
    ffn_back_part = matmul_nt(grad_hidden, up_full)
    ffn_back_low = matmul_nt(grad_hidden, up_second_flattened)
    back_here, back_low_here = scatter_rows((ffn_back_part, ffn_back_low))
    up_back_here = (back_low_here * select_here).astype(jnp.bfloat16)
    grad_second = back_here + matmul_nt(up_back_here, up_first_flattened)
    grad_middle_here = grad_top_here + second_back(grad_second)[0]
    grad_middle_low_here = grad_middle_here.astype(jnp.bfloat16)
    heads_back_here = (
        matmul_nt(grad_middle_low_here, heads_second_flattened) * select_here
    ).astype(jnp.bfloat16)
    up_back, heads_back = gather_rows((up_back_here, heads_back_here))
    down_second_gradient = matmul_tn(down_low, grad_top_low)
    grad_up_in = matmul_tn(second_act, up_back)
    heads_second_gradient = matmul_tn(heads_low_here, grad_middle_low_here)
    grad_heads_in = matmul_tn(heads_act, heads_back)
    grad_heads_here = (
        matmul_nt(grad_middle_low_here, heads_full)
        + matmul_nt(heads_back_here, heads_first_all_flattened)
    ).astype(jnp.bfloat16)
    grad_heads = lax.all_to_all(grad_heads_here, "tp", 1, 0, tiled=True)
    grad_heads_wide = grad_heads.reshape(seq_here, local_len, device_heads, head_width).astype(
        jnp.float32
    )
    scaled_grad = (grad_heads_wide / per_total).astype(jnp.bfloat16)
    row_delta = jnp.sum(grad_heads_wide * heads_raw, axis=-1) / per_total[..., 0]
    grad_queries, grad_keyrows, grad_valrows = block_grads(
        queries,
        scaled_grad,
        row_delta,
        piece_keys,
        piece_values,
        here_pos,
        key_pos,
        visible_mask,
        slopes,
    )
    grad_keys_all, grad_values_all = (
        lax.psum_scatter(grad_keyrows, "ctx", scatter_dimension=1, tiled=True),
        lax.psum_scatter(grad_valrows, "ctx", scatter_dimension=1, tiled=True),
    )
    grad_projected = jnp.concatenate(
        [
            grad_queries.reshape(tok_rows, local_width),
            grad_keys_all.reshape(tok_rows, local_width),
            grad_values_all.reshape(tok_rows, local_width),
        ],
        axis=1,
    ).astype(jnp.bfloat16)
    projection_second_gradient = matmul_tn(first_low, grad_projected)
    attn_back_part = matmul_nt(grad_projected, qkv_full)
    attn_back_low = matmul_nt(grad_projected, projection_second_flattened)
    first_here, first_low_here = scatter_rows((attn_back_part, attn_back_low))
    qkv_back_here = (first_low_here * select_here).astype(jnp.bfloat16)
    grad_first = first_here + matmul_nt(qkv_back_here, projection_first_flattened)
    input_here = (grad_middle_here + first_back_full(grad_first)[0]).astype(jnp.bfloat16)
    input_rows, qkv_back = gather_rows((input_here, qkv_back_here))
    input_grad = input_rows.reshape(layer_input.shape)
    grad_qkv_in = matmul_tn(first_act, qkv_back)
    heads_second_total = lax.psum(heads_second_gradient, "tp")
    adapter_terms = (
        unflat_in(grad_qkv_in, adapter_tables),
        projection_second_gradient.reshape(adapter_projection_second.shape),
        unflat_in(grad_heads_in, adapter_tables),
        heads_second_total.reshape(adapter_heads_second.shape),
        unflat_in(grad_up_in, adapter_tables),
        up_second_gradient.reshape(adapter_up_second.shape),
        unflat_in(grad_down_in, adapter_tables),
        down_second_gradient.reshape(adapter_down_second.shape),
    )
    summed = lax.psum(adapter_terms, ("shard", "ctx"))
    return (
        layer_out,
        input_grad,
        summed[0],
        summed[1],
        summed[2],
        summed[3],
        summed[4],
        summed[5],
        summed[6],
        summed[7],
    )


def solution(mesh):
    placed = (
        P("shard", "ctx", None),
        P("shard", "ctx", None),
        P("shard", None),
        P("shard"),
        P(),
        P(),
        P(),
        P(),
        P("shard", None, "tp"),
        P("tp", "shard"),
        P("shard", "tp"),
        P("tp", "shard"),
        P(),
        P(None, None, None, "tp"),
        P(None, "tp", None),
        P(),
        P(),
        P(None, None, "tp"),
        P(None, "tp", None),
        P(),
    )
    return jax.shard_map(
        body,
        mesh=mesh,
        in_specs=placed,
        out_specs=(
            P("shard", "ctx", None),
            P("shard", "ctx", None),
            P(),
            P(None, None, None, "tp"),
            P(None, "tp", None),
            P(),
            P(),
            P(None, None, "tp"),
            P(None, "tp", None),
            P(),
        ),
        check_vma=False,
    )
```

profile of v0, /device:TPU:0, one launch (start us, length us, event | category | flops | bytes accessed | tf_op | source)
XLA Modules:
  0.0 1514.2 jit_solution(5506899695237392603)
XLA Ops:
  7.2 4.7 copy.75
  13.4 3.2 convert_reduce_fusion
  23.0 8.6 all-gather.11.cloned.1.call-done
  31.6 10.1 fusion.40
  45.4 69.8 %all-gather.17.cloned.1.call-done = bf16[2048,1024]{1,0:T(8,128)(2,1)} async-done(((bf16[512,1024]{1,0:T(8,128)(2,1)}), bf16[2048,1024]{1,0:T(8,128)(2,1)}) %all-gather.17.cloned.1.call-update) | async-done | bytes 4194320 | tf_op jit(solution)/shard_map/all_gather | solution.py:177
  117.2 2.6 broadcast_multiply_fusion
  123.6 45.1 %all-gather.13.cloned.1.call-done = bf16[4,1024,512]{2,1,0:T(8,128)(2,1)} async-done(((bf16[4,256,512]{2,1,0:T(8,128)(2,1)}), bf16[4,1024,512]{2,1,0:T(8,128)(2,1)}) %all-gather.13.cloned.1.call-update) | async-done | bytes 4194320 | tf_op jit(solution)/shard_map/all_gather | solution.py:216
  168.7 6.3 copy.77
  175.0 48.4 %all-gather.15.cloned.1.call-done = bf16[4,1024,512]{1,2,0:T(8,128)(2,1)} async-done(((bf16[4,256,512]{1,2,0:T(8,128)(2,1)}), bf16[4,1024,512]{1,2,0:T(8,128)(2,1)}) %all-gather.15.cloned.1.call-update) | async-done | bytes 4194320 | tf_op jit(solution)/shard_map/all_gather | solution.py:215
  223.4 14.3 fusion.37
  237.7 11.8 fusion.38
  249.5 4.6 all-to-all-start
  254.1 8.5 convert.22
  262.6 27.4 %all_gather.41 = bf16[8,2048,16]{1,2,0:T(8,128)(2,1)S(1)} all-gather(bf16[8,512,16]{1,2,0:T(8,128)(2,1)S(1)} %copy-done.44), channel_id=1, replica_groups=mesh['shard'=2,'ctx'=4,'tp'=4] {'tp'}, dimensions={1}, use_global_device_ids=true | all-gather | bytes 655360 | tf_op jit(solution)/shard_map/all_gather | solution.py:182
  290.6 6.4 convolution_add_fusion.6
  299.5 3.6 fusion.23
  303.1 14.9 fusion.44
  317.9 62.5 %all-gather.21.cloned.1.call-done = bf16[1024,2048]{1,0:T(8,128)(2,1)} async-done(((bf16[256,2048]{1,0:T(8,128)(2,1)}), bf16[1024,2048]{1,0:T(8,128)(2,1)}) %all-gather.21.cloned.1.call-update) | async-done | bytes 4194320 | tf_op jit(solution)/shard_map/all_gather | solution.py:124
  380.4 15.4 %fusion.41 = f32[1024,2048]{1,0:T(8,128)} fusion(bf16[1024,2048]{1,0:T(8,128)(2,1)} %all-gather.21.cloned.1.call-done, bf16[2048,2048]{1,0:T(8,128)(2,1)} %all-gather.23.cloned.1.call-done), kind=kOutput, calls=%fused_computation.122 | convolution fusion | flops 8589934592 | bytes 20971520 | tf_op jit(solution)/shard_map/dot_general | solution.py:41
  397.1 6.9 multiply_convert_fusion.1
  404.0 9.6 fusion.3
  415.7 8.9 fusion.45
  424.5 4.2 pad_maximum_fusion.1
  429.2 151.1 %reduce-scatter.8.cloned.1.call-done = f32[256,2176]{1,0:T(8,128)} async-done(((f32[1024,2176]{1,0:T(8,128)}), f32[256,2176]{1,0:T(8,128)}) %reduce-scatter.8.cloned.1.call-update) | async-done | bytes 2228240 | tf_op jit(solution)/shard_map/reduce_scatter | solution.py:116
  581.3 2.4 multiply_reduce_fusion.4
  587.9 2.4 fusion.47
  593.9 30.1 %all_to_all.29 = bf16[256,4,512]{0,2,1:T(8,128)(2,1)S(1)} all-to-all(bf16[256,4,512]{0,2,1:T(8,128)(2,1)} %bitcast.197), channel_id=1, replica_groups=mesh['shard'=2,'ctx'=4,'tp'=4] {'tp'}, dimensions={1} | all-to-all | bytes 2097152 | tf_op jit(solution)/shard_map/all_to_all | solution.py:285
  627.5 9.2 multiply_convert_fusion
  636.7 3.3 copy-done.2
  640.0 4.9 multiply_bitcast_fusion
  645.0 11.7 fusion.10
  656.9 3.8 fusion.43
  660.8 11.3 fusion.42
  672.1 4.2 pad_maximum_fusion
  676.4 9.0 fusion.19
  685.4 2.4 copy.87
  687.7 2.5 bitcast_dynamic-update-slice_fusion.2
  690.2 40.2 %reduce-scatter.10.cloned.1.call-done = f32[4,256,4,128]{1,3,2,0:T(8,128)} async-done(((f32[4,1024,4,128]{1,3,2,0:T(8,128)}), f32[4,256,4,128]{1,3,2,0:T(8,128)}) %reduce-scatter.10.cloned.1.call-update) | async-done | bytes 2097168 | tf_op jit(solution)/shard_map/reduce_scatter | solution.py:303
  730.4 2.7 convert.17
  733.1 2.3 copy.89
  735.5 84.4 %reduce-scatter.12.cloned.1.call-done = f32[4,256,4,128]{1,3,2,0:T(8,128)} async-done(((f32[4,1024,4,128]{1,3,2,0:T(8,128)}), f32[4,256,4,128]{1,3,2,0:T(8,128)}) %reduce-scatter.12.cloned.1.call-update) | async-done | bytes 2097168 | tf_op jit(solution)/shard_map/reduce_scatter | solution.py:304
  819.8 2.7 convert.18
  824.9 2.4 bitcast_dynamic-update-slice_fusion.1
  827.3 2.7 bitcast_dynamic-update-slice_fusion
  830.0 3.0 fusion.49
  833.0 8.8 fusion.48
  841.8 4.2 pad_maximum_fusion.2
  848.1 126.9 %reduce-scatter.6.cloned.1.call-done = f32[256,2176]{1,0:T(8,128)} async-done(((f32[1024,2176]{1,0:T(8,128)}), f32[256,2176]{1,0:T(8,128)}) %reduce-scatter.6.cloned.1.call-update) | async-done | bytes 2228240 | tf_op jit(solution)/shard_map/reduce_scatter | solution.py:116
  975.0 156.1 %reduce-scatter.14.cloned.1.call-done = f32[256,2176]{1,0:T(8,128)} async-done(((f32[1024,2176]{1,0:T(8,128)}), f32[256,2176]{1,0:T(8,128)}) %reduce-scatter.14.cloned.1.call-update) | async-done | bytes 2228240 | tf_op jit(solution)/shard_map/reduce_scatter | solution.py:116
  1132.1 3.0 multiply_reduce_fusion.2
  1135.1 2.4 fusion.34
  1145.9 4.2 fusion.52
  1151.9 24.1 %all_gather.47 = bf16[1024,256]{1,0:T(8,128)(2,1)S(1)} all-gather(bf16[256,256]{1,0:T(8,128)(2,1)S(1)} %pad_maximum_fusion.5), channel_id=1, replica_groups=mesh['shard'=2,'ctx'=4,'tp'=4] {'tp'}, dimensions={0}, use_global_device_ids=true | all-gather | bytes 655360 | tf_op jit(solution)/shard_map/all_gather | solution.py:124
  1178.5 3.9 fusion.26
  1182.4 2.5 fusion.50
  1186.5 48.3 %all-gather.29.cloned.1.call-done = bf16[1024,2176]{1,0:T(8,128)(2,1)} async-done(((bf16[256,2176]{1,0:T(8,128)(2,1)}), bf16[1024,2176]{1,0:T(8,128)(2,1)}) %all-gather.29.cloned.1.call-update) | async-done | bytes 4456464 | tf_op jit(solution)/shard_map/all_gather | solution.py:124
  1235.8 84.0 %all-gather.27.cloned.1.call-done = bf16[1024,2176]{1,0:T(8,128)(2,1)} async-done(((bf16[256,2176]{1,0:T(8,128)(2,1)}), bf16[1024,2176]{1,0:T(8,128)(2,1)}) %all-gather.27.cloned.1.call-update) | async-done | bytes 4456464 | tf_op jit(solution)/shard_map/all_gather | solution.py:124
  1321.1 4.0 fusion.54
  1326.8 46.1 %all-reduce.4.cloned.1.call-done = f32[8,16,2048]{2,1,0:T(8,128)} async-done(((f32[8,16,2048]{2,1,0:T(8,128)}), f32[8,16,2048]{2,1,0:T(8,128)}) %all-reduce.4.cloned.1.call-update) | async-done | bytes 1048592 | tf_op jit(solution)/shard_map/psum | solution.py:324
  1373.0 4.9 slice.65
  1377.9 2.6 slice.70
  1380.5 115.5 %all-reduce.6.cloned.1.call-done = (f32[8,2048,16]{1,2,0:T(8,128)}, f32[8,16,3,512]{3,2,1,0:T(4,128)}, f32[8,512,16]{1,2,0:T(8,128)}, f32[8,16,2048]{2,1,0:T(8,1...) async-done(((f32[8,2048,16]{1,2,0:T(8,128)}, f32[8,16,3,512]{3,2,1,0:T(4,128)}, ...) | async-done | bytes 7340048 | tf_op jit(solution)/shard_map/psum | solution.py:335
  1496.0 2.5 copy.96
  1498.5 2.4 copy.123
  (234 shorter events, 66.4 us)
Async XLA Ops:
  7.2 389.8 %copy-start = (bf16[8,16,2048]{2,1,0:T(8,128)(2,1)S(1)}, bf16[8,16,2048]{2,1,0:T(8,128)(2,1)}, u32[]{:S(2)}) copy-start(bf16[8,16,2048]{2,1,0:T(8,128)(2,1)} %param.37) | copy-start | bytes 1572868
  7.2 5.6 copy-start.43
  7.2 24.4 %all-gather.11.cloned.1.call-start = ((), (), s32[]{:S(2)}) async-start(), calls=%async_computation.7 | async-start | bytes 9437184 | tf_op jit(solution)/shard_map/all_gather | solution.py:200
  12.0 103.2 %all-gather.17.cloned.1.call-start = ((), (), s32[]{:S(2)}) async-start(), calls=%async_computation.10 | async-start | bytes 5242880 | tf_op jit(solution)/shard_map/all_gather | solution.py:177
  12.8 155.9 %all-gather.13.cloned.1.call-start = ((), (), s32[]{:S(2)}) async-start(), calls=%async_computation.8 | async-start | bytes 5242880 | tf_op jit(solution)/shard_map/all_gather | solution.py:216
  12.8 3.8 copy-start.3
  13.3 28.4 %copy-start.20 = (bf16[16,8,3,512]{3,1,2,0:T(8,128)(2,1)}, bf16[16,8,3,512]{3,1,2,0:T(8,128)(2,1)S(1)}, u32[]{:S(2)}) copy-start(bf16[16,8,3,512]{3,1,2,0:T(8,128)(2,1)S(1)} %copy.105) | copy-start | bytes 1179652
  13.4 4.5 copy-start.46
  13.4 4.5 copy-start.51
  17.9 3.8 copy-start.26
  23.0 18.7 %copy-start.22 = (bf16[1024,128]{1,0:T(8,128)(2,1)}, bf16[1024,128]{1,0:T(8,128)(2,1)S(1)}, u32[]{:S(2)}) copy-start(bf16[1024,128]{1,0:T(8,128)(2,1)S(1)} %fusion.21) | copy-start | bytes 786436
  44.0 179.4 %all-gather.15.cloned.1.call-start = ((), (), s32[]{:S(2)}) async-start(), calls=%async_computation.9 | async-start | bytes 5242880 | tf_op jit(solution)/shard_map/all_gather | solution.py:215
  45.3 245.2 %all-gather.19.cloned.1.call-start = ((), (), s32[]{:S(2)}) async-start(), calls=%async_computation.11 | async-start | bytes 12582912 | tf_op jit(solution)/shard_map/all_gather | solution.py:176
  115.2 187.9 %all-gather.25.cloned.1.call-start = ((), (), s32[]{:S(2)}) async-start(), calls=%async_computation.14 | async-start | bytes 12582912 | tf_op jit(solution)/shard_map/all_gather | solution.py:205
  115.8 202.1 %all-gather.23.cloned.1.call-start = ((), (), s32[]{:S(2)}) async-start(), calls=%async_computation.13 | async-start | bytes 12582912 | tf_op jit(solution)/shard_map/all_gather | solution.py:201
  123.6 99.8 %copy-start.14 = (bf16[4,256,4,128]{1,3,2,0:T(8,128)(2,1)}, bf16[4,256,4,128]{1,3,2,0:T(8,128)(2,1)S(1)}, u32[]{:S(2)}) copy-start(bf16[4,256,4,128]{1,3,2,0:T(8,128)(2,1)S(1)} %copy.88) | copy-start | bytes 3145732
  223.4 14.3 copy-start.4
  249.5 40.5 %all-to-all-start = ((bf16[4,256,512]{1,2,0:T(8,128)(2,1)}), bf16[4,256,512]{1,2,0:T(8,128)(2,1)S(1)}, u32[]{:S(2)}, u32[]{:S(2)}) async-start(bf16[4,256,512]{1,2,0:T(8,128)(2,1)} %bitcast.12), calls=%async_computation | async-start | bytes 2097152 | tf_op jit(solution)/shard_map/all_to_all | solution.py:235
  254.1 126.2 %all-gather.21.cloned.1.call-start = ((), (), s32[]{:S(2)}) async-start(), calls=%async_computation.12 | async-start | bytes 5242880 | tf_op jit(solution)/shard_map/all_gather | solution.py:124
  254.1 8.5 copy-start.44
  290.1 6.9 copy-start.18
  290.6 6.5 copy-start.40
  290.6 6.5 copy-start.29
  299.4 281.0 %reduce-scatter.8.cloned.1.call-start = ((), (), s32[]{:S(2)}) async-start(), calls=%async_computation.17 | async-start | bytes 11141120 | tf_op jit(solution)/shard_map/reduce_scatter | solution.py:116
  380.4 15.4 %copy-start.6 = (bf16[1024,2048]{1,0:T(8,128)(2,1)S(1)}, bf16[1024,2048]{1,0:T(8,128)(2,1)}, u32[]{:S(2)}) copy-start(bf16[1024,2048]{1,0:T(8,128)(2,1)} %all-gather.21.cloned.1.call-done) | copy-start | bytes 12582916
  380.4 15.4 %copy-start.24 = (bf16[8,2048,16]{1,2,0:T(8,128)(2,1)S(1)}, bf16[8,2048,16]{1,2,0:T(8,128)(2,1)}, u32[]{:S(2)}) copy-start(bf16[8,2048,16]{1,2,0:T(8,128)(2,1)} %param.36) | copy-start | bytes 1572868
  397.0 7.0 copy-start.31
  397.0 6.9 copy-start.42
  397.0 18.6 %slice-start.4 = ((s8[8388608]{0:T(1024)(128)(4,1)}), s8[4194304]{0:T(1024)(128)(4,1)S(1)}, s32[]{:S(2)}) async-start(s8[8388608]{0:T(1024)(128)(4,1)} %bitcast.221), calls=%async_computation.28 | async-start | bytes 8388608
  404.0 11.7 slice-start.5
  428.8 152.5 %copy-start.25 = (bf16[8,2048,16]{1,2,0:T(8,128)(2,1)S(1)}, bf16[8,2048,16]{1,2,0:T(8,128)(2,1)}, u32[]{:S(2)}) copy-start(bf16[8,2048,16]{1,2,0:T(8,128)(2,1)} %param.36) | copy-start | bytes 1572868
  428.8 301.6 %reduce-scatter.10.cloned.1.call-start = ((), (), s32[]{:S(2)}) async-start(), calls=%async_computation.18 | async-start | bytes 10485760 | tf_op jit(solution)/shard_map/reduce_scatter | solution.py:303
  581.3 6.5 slice-start
  583.7 3.7 copy-start.30
  583.7 4.2 slice-start.1
  627.5 12.5 copy-start.15
  636.7 3.3 copy-start.2
  644.9 174.9 %reduce-scatter.12.cloned.1.call-start = ((), (), s32[]{:S(2)}) async-start(), calls=%async_computation.19 | async-start | bytes 10485760 | tf_op jit(solution)/shard_map/reduce_scatter | solution.py:304
  656.7 318.3 %reduce-scatter.6.cloned.1.call-start = ((), (), s32[]{:S(2)}) async-start(), calls=%async_computation.15 | async-start | bytes 11141120 | tf_op jit(solution)/shard_map/reduce_scatter | solution.py:116
  656.9 3.9 copy-start.7
  676.3 454.7 %reduce-scatter.14.cloned.1.call-start = ((), (), s32[]{:S(2)}) async-start(), calls=%async_computation.20 | async-start | bytes 11141120 | tf_op jit(solution)/shard_map/reduce_scatter | solution.py:116
  735.5 94.5 %copy-start.21 = (bf16[16,8,3,512]{3,1,2,0:T(8,128)(2,1)S(1)}, bf16[16,8,3,512]{3,1,2,0:T(8,128)(2,1)}, u32[]{:S(2)}) copy-start(bf16[16,8,3,512]{3,1,2,0:T(8,128)(2,1)} %copy-done.20) | copy-start | bytes 1179652
  830.0 3.0 copy-start.5
  846.0 286.1 %copy-start.27 = (bf16[8,2048,16]{1,2,0:T(8,128)(2,1)S(1)}, bf16[8,2048,16]{1,2,0:T(8,128)(2,1)}, u32[]{:S(2)}) copy-start(bf16[8,2048,16]{1,2,0:T(8,128)(2,1)} %param.32) | copy-start | bytes 1572868
  846.0 286.1 %copy-start.47 = (f32[2048]{0:T(1024)S(1)}, f32[2048]{0:T(1024)}, u32[]{:S(2)}) copy-start(f32[2048]{0:T(1024)} %param.24) | copy-start | bytes 24580
  846.0 388.8 %all-gather.29.cloned.1.call-start = ((), (), s32[]{:S(2)}) async-start(), calls=%async_computation.21 | async-start | bytes 5570560 | tf_op jit(solution)/shard_map/all_gather | solution.py:124
  1137.5 3.0 copy-start.28
  1140.5 179.3 %all-gather.27.cloned.1.call-start = ((), (), s32[]{:S(2)}) async-start(), calls=%async_computation.16 | async-start | bytes 5570560 | tf_op jit(solution)/shard_map/all_gather | solution.py:124
  1142.6 3.3 copy-start.32
  1143.7 229.2 %all-reduce.4.cloned.1.call-start = ((), (), s32[]{:S(2)}) async-start(), calls=%async_computation.22 | async-start | bytes 2097152 | tf_op jit(solution)/shard_map/psum | solution.py:324
  1145.9 4.2 copy-start.8
  1151.8 25.3 %copy-start.17 = (bf16[256,2048]{1,0:T(8,128)(2,1)S(1)}, bf16[256,2048]{1,0:T(8,128)(2,1)}, u32[]{:S(2)}) copy-start(bf16[256,2048]{1,0:T(8,128)(2,1)} %copy-done.16) | copy-start | bytes 3145732
  1151.8 25.3 %copy-start.41 = (bf16[256,128]{1,0:T(8,128)(2,1)S(1)}, bf16[256,128]{1,0:T(8,128)(2,1)}, u32[]{:S(2)}) copy-start(bf16[256,128]{1,0:T(8,128)(2,1)} %copy-done.40) | copy-start | bytes 196612
  1177.1 5.3 copy-start.23
  1178.5 317.5 %all-reduce.6.cloned.1.call-start = ((), (), s32[]{:S(2)}) async-start(), calls=%async_computation.23 | async-start | bytes 15204352 | tf_op jit(solution)/shard_map/psum | solution.py:335
  1321.1 4.0 copy-start.10
  1372.9 5.0 slice-start.2
  1373.0 5.0 slice-start.3
  1496.0 6.6 copy-start.37
  1496.0 7.5 copy-start.36
  1496.0 8.5 copy-start.35
  1498.5 7.0 copy-start.34
  1502.6 3.9 copy-start.33
  1502.6 4.9 copy-start.1
  (14 other events, 25.7 us)
Sparse Core Ops, SparseCore 0:
  12.1 19.4 all-gather.10
  33.2 81.9 all-gather.16
  117.6 51.0 all-gather.12
  170.9 52.4 all-gather.14
  224.8 19.8 all-gather.18
  246.1 21.0 all-gather.24
  268.7 21.0 all-gather.22
  299.5 80.7 all-gather.20
  428.9 151.4 reduce-scatter.7
  645.0 85.3 reduce-scatter.9
  733.5 86.3 reduce-scatter.11
  822.1 152.8 reduce-scatter.5
  977.3 153.7 reduce-scatter.13
  1140.6 94.1 all-gather.28
  1236.2 83.5 all-gather.26
  1322.6 50.3 all-reduce.3
  1378.1 117.8 all-reduce.5
where the time goes:
time: 1520 us; the launch traced here: 1510 us
  waiting for transfers between devices  1090 us (72%)
  matrix products  201 us (13%)
  blocking collectives  81.7 us (5%)
  local copies, waits for them, and re-layouts  66.4 us (4%)
  other arithmetic  54.7 us (4%)
    reduce_scatter x3, waiting for transfers between devices, scatter_rows(): lax.psum_scatter(jnp.concatenate(partials, axis=1), 'tp', scatter_dimensi...  434 us
    all_gather x3, waiting for transfers between devices, gather_rows(): lax.all_gather(jnp.concatenate(rows_here, axis=1), 'tp', axis=0, tiled=True)  195 us
    psum x1, waiting for transfers between devices, body(): summed = lax.psum(adapter_terms, ('shard', 'ctx'))  115 us
    reduce_scatter x1, waiting for transfers between devices, body(): lax.psum_scatter(grad_valrows, 'ctx', scatter_dimension=1, tiled=True)  84.4 us
    all_gather x1, waiting for transfers between devices, body(): lax.all_gather(attention_output_weight, 'tp', axis=0, tiled=True)  69.8 us
    dot_general x12, matrix products, matmul(): return jnp.dot(left_mat, right_mat, preferred_element_type=jnp.float32)  60.3 us
    dot_general x12, matrix products, matmul_nt(): lax.dot_general(left_mat, right_mat, (((1,), (1,)), ((), ())), preferred_...  59.5 us
    all_gather x1, waiting for transfers between devices, body(): lax.all_gather(key_rows, 'ctx', axis=1, tiled=True)  48.4 us
  transfers between devices with their start and end apart: 18, of which 14 were waited for; matrix products, arithmetic and copies ran while one was open for 14% of the time, Pallas kernels for 0%

commit v1 on v0

--- a/solution.py
+++ b/solution.py
@@ -321,7 +321,11 @@
     input_rows, qkv_back = gather_rows((input_here, qkv_back_here))
     input_grad = input_rows.reshape(layer_input.shape)
     grad_qkv_in = matmul_tn(first_act, qkv_back)
-    heads_second_total = lax.psum(heads_second_gradient, "tp")
+    heads_second_total = heads_second_gradient
+    for hop in (1, 2):
+        heads_second_total = heads_second_total + lax.ppermute(
+            heads_second_total, "tp", [(dev, dev ^ hop) for dev in range(4)]
+        )
     adapter_terms = (
         unflat_in(grad_qkv_in, adapter_tables),
         projection_second_gradient.reshape(adapter_projection_second.shape),

time: 1520 us -> 1510 us (level)
  waiting for transfers between devices: 1090 us -> 994 us
  blocking collectives: 81.7 us -> 158 us
    all_gather x3, waiting for transfers between devices: 195 us -> 86.7 us  [gather_rows(): lax.all_gather(jnp.concatenate(rows_here, axis=1), 'tp', axis=0, tiled=True)]
    all_gather x1, blocking collectives: 24.1 us -> 100 us  [gather_rows(): lax.all_gather(jnp.concatenate(rows_here, axis=1), 'tp', axis=0, tiled=True)]
    ppermute x0 -> x2, waiting for transfers between devices: none -> 66.2 us  [body(): lax.ppermute(heads_second_total, 'tp', [(dev, dev ^ hop) for dev in range...]
    psum x1 -> x0, waiting for transfers between devices: 46.1 us -> none  [body(): heads_second_total = lax.psum(heads_second_gradient, 'tp')]
  transfers between devices with their start and end apart: 18 -> 19, of which waited for: 14 -> 13; matrix products, arithmetic and copies ran while one was open for 14% -> 14% of each run, Pallas kernels for 0% -> 0%
where the time goes in v1:
time: 1510 us; the launch traced here: 1500 us
  waiting for transfers between devices  994 us (66%)
  matrix products  199 us (13%)
  blocking collectives  158 us (10%)
  local copies, waits for them, and re-layouts  68 us (5%)
  other arithmetic  57.1 us (4%)
  between operations  15.1 us (1%)
    reduce_scatter x3, waiting for transfers between devices, scatter_rows(): lax.psum_scatter(jnp.concatenate(partials, axis=1), 'tp', scatter_dimensi...  434 us
    psum x1, waiting for transfers between devices, body(): summed = lax.psum(adapter_terms, ('shard', 'ctx'))  109 us
    all_gather x1, blocking collectives, gather_rows(): lax.all_gather(jnp.concatenate(rows_here, axis=1), 'tp', axis=0, tiled=True)  100 us
    all_gather x3, waiting for transfers between devices, gather_rows(): lax.all_gather(jnp.concatenate(rows_here, axis=1), 'tp', axis=0, tiled=True)  86.7 us
    reduce_scatter x1, waiting for transfers between devices, body(): lax.psum_scatter(grad_valrows, 'ctx', scatter_dimension=1, tiled=True)  84.4 us
    all_gather x1, waiting for transfers between devices, body(): lax.all_gather(attention_output_weight, 'tp', axis=0, tiled=True)  69.8 us
    ppermute x2, waiting for transfers between devices, body(): lax.ppermute(heads_second_total, 'tp', [(dev, dev ^ hop) for dev in range...  66.2 us
    dot_general x12, matrix products, matmul(): return jnp.dot(left_mat, right_mat, preferred_element_type=jnp.float32)  60.4 us
  transfers between devices with their start and end apart: 19, of which 13 were waited for; matrix products, arithmetic and copies ran while one was open for 14% of the time, Pallas kernels for 0%

profile of v1, /device:TPU:0, one launch (start us, length us, event | category | flops | bytes accessed | tf_op | source)
XLA Modules:
  0.0 1503.5 jit_solution(6230461259534484888)
XLA Ops:
  7.2 4.7 copy.75
  13.4 3.2 convert_reduce_fusion
  23.0 8.6 all-gather.11.cloned.1.call-done
  31.6 10.1 fusion.40
  45.4 69.8 %all-gather.17.cloned.1.call-done = bf16[2048,1024]{1,0:T(8,128)(2,1)} async-done(((bf16[512,1024]{1,0:T(8,128)(2,1)}), bf16[2048,1024]{1,0:T(8,128)(2,1)}) %all-gather.17.cloned.1.call-update) | async-done | bytes 4194320 | tf_op jit(solution)/shard_map/all_gather | solution.py:177
  117.2 2.6 broadcast_multiply_fusion
  123.6 45.1 %all-gather.13.cloned.1.call-done = bf16[4,1024,512]{2,1,0:T(8,128)(2,1)} async-done(((bf16[4,256,512]{2,1,0:T(8,128)(2,1)}), bf16[4,1024,512]{2,1,0:T(8,128)(2,1)}) %all-gather.13.cloned.1.call-update) | async-done | bytes 4194320 | tf_op jit(solution)/shard_map/all_gather | solution.py:216
  168.7 6.3 copy.77
  175.0 48.4 %all-gather.15.cloned.1.call-done = bf16[4,1024,512]{1,2,0:T(8,128)(2,1)} async-done(((bf16[4,256,512]{1,2,0:T(8,128)(2,1)}), bf16[4,1024,512]{1,2,0:T(8,128)(2,1)}) %all-gather.15.cloned.1.call-update) | async-done | bytes 4194320 | tf_op jit(solution)/shard_map/all_gather | solution.py:215
  223.4 14.3 fusion.37
  237.7 11.8 fusion.38
  249.5 4.6 all-to-all-start
  254.1 8.5 convert.22
  262.6 27.4 %all_gather.41 = bf16[8,2048,16]{1,2,0:T(8,128)(2,1)S(1)} all-gather(bf16[8,512,16]{1,2,0:T(8,128)(2,1)S(1)} %copy-done.45), channel_id=1, replica_groups=mesh['shard'=2,'ctx'=4,'tp'=4] {'tp'}, dimensions={1}, use_global_device_ids=true | all-gather | bytes 655360 | tf_op jit(solution)/shard_map/all_gather | solution.py:182
  290.6 6.4 convolution_add_fusion.6
  299.5 3.6 fusion.23
  303.1 15.1 %fusion.44 = f32[1024,2048]{1,0:T(8,128)} fusion(bf16[1024,2048]{1,0:T(8,128)(2,1)} %bitcast.164, bf16[2048,2048]{1,0:T(8,128)(2,1)} %all-gather.25.cloned.1.call-done), kind=kOutput, calls=%fused_computation.125 | convolution fusion | flops 8589934592 | bytes 20971520 | tf_op jit(solution)/shard_map/dot_general | solution.py:51
  318.1 62.3 %all-gather.21.cloned.1.call-done = bf16[1024,2048]{1,0:T(8,128)(2,1)} async-done(((bf16[256,2048]{1,0:T(8,128)(2,1)}), bf16[1024,2048]{1,0:T(8,128)(2,1)}) %all-gather.21.cloned.1.call-update) | async-done | bytes 4194320 | tf_op jit(solution)/shard_map/all_gather | solution.py:124
  380.4 15.5 %fusion.41 = f32[1024,2048]{1,0:T(8,128)} fusion(bf16[1024,2048]{1,0:T(8,128)(2,1)} %all-gather.21.cloned.1.call-done, bf16[2048,2048]{1,0:T(8,128)(2,1)} %all-gather.23.cloned.1.call-done), kind=kOutput, calls=%fused_computation.122 | convolution fusion | flops 8589934592 | bytes 20971520 | tf_op jit(solution)/shard_map/dot_general | solution.py:41
  397.2 6.9 multiply_convert_fusion.1
  404.1 9.6 fusion.3
  415.8 8.9 fusion.45
  424.7 4.2 pad_maximum_fusion.1
  429.3 151.1 %reduce-scatter.8.cloned.1.call-done = f32[256,2176]{1,0:T(8,128)} async-done(((f32[1024,2176]{1,0:T(8,128)}), f32[256,2176]{1,0:T(8,128)}) %reduce-scatter.8.cloned.1.call-update) | async-done | bytes 2228240 | tf_op jit(solution)/shard_map/reduce_scatter | solution.py:116
  581.4 2.4 multiply_reduce_fusion.4
  588.0 2.4 fusion.47
  594.0 30.1 %all_to_all.29 = bf16[256,4,512]{0,2,1:T(8,128)(2,1)S(1)} all-to-all(bf16[256,4,512]{0,2,1:T(8,128)(2,1)} %bitcast.196), channel_id=1, replica_groups=mesh['shard'=2,'ctx'=4,'tp'=4] {'tp'}, dimensions={1} | all-to-all | bytes 2097152 | tf_op jit(solution)/shard_map/all_to_all | solution.py:285
  627.6 9.2 multiply_convert_fusion
  636.8 3.3 copy-done.2
  640.0 4.9 multiply_bitcast_fusion
  645.0 11.6 fusion.10
  656.9 3.8 fusion.43
  660.9 11.3 fusion.42
  672.1 4.2 pad_maximum_fusion
  676.4 9.0 fusion.19
  685.4 2.4 copy.87
  687.8 2.5 bitcast_dynamic-update-slice_fusion.2
  690.3 40.2 %reduce-scatter.10.cloned.1.call-done = f32[4,256,4,128]{1,3,2,0:T(8,128)} async-done(((f32[4,1024,4,128]{1,3,2,0:T(8,128)}), f32[4,256,4,128]{1,3,2,0:T(8,128)}) %reduce-scatter.10.cloned.1.call-update) | async-done | bytes 2097168 | tf_op jit(solution)/shard_map/reduce_scatter | solution.py:303
  730.5 2.7 convert.17
  733.2 2.3 copy.89
  735.5 84.4 %reduce-scatter.12.cloned.1.call-done = f32[4,256,4,128]{1,3,2,0:T(8,128)} async-done(((f32[4,1024,4,128]{1,3,2,0:T(8,128)}), f32[4,256,4,128]{1,3,2,0:T(8,128)}) %reduce-scatter.12.cloned.1.call-update) | async-done | bytes 2097168 | tf_op jit(solution)/shard_map/reduce_scatter | solution.py:304
  819.9 2.7 convert.18
  822.6 2.3 copy.90
  824.9 2.4 bitcast_dynamic-update-slice_fusion.1
  827.4 2.7 bitcast_dynamic-update-slice_fusion
  830.1 3.0 fusion.49
  833.1 8.8 fusion.48
  841.9 4.2 pad_maximum_fusion.2
  848.2 126.9 %reduce-scatter.6.cloned.1.call-done = f32[256,2176]{1,0:T(8,128)} async-done(((f32[1024,2176]{1,0:T(8,128)}), f32[256,2176]{1,0:T(8,128)}) %reduce-scatter.6.cloned.1.call-update) | async-done | bytes 2228240 | tf_op jit(solution)/shard_map/reduce_scatter | solution.py:116
  975.1 156.1 %reduce-scatter.14.cloned.1.call-done = f32[256,2176]{1,0:T(8,128)} async-done(((f32[1024,2176]{1,0:T(8,128)}), f32[256,2176]{1,0:T(8,128)}) %reduce-scatter.14.cloned.1.call-update) | async-done | bytes 2228240 | tf_op jit(solution)/shard_map/reduce_scatter | solution.py:116
  1132.2 3.0 multiply_reduce_fusion.2
  1135.2 2.4 fusion.34
  1149.6 4.3 fusion.52
  1155.7 66.2 %collective-permute-done = f32[128,2048]{1,0:T(8,128)} collective-permute-done((f32[128,2048]{1,0:T(8,128)S(1)}, f32[128,2048]{1,0:T(8,128)}, u32[]{:S(2)}, u32[]{:S(2)}) %collective-permute-start) | collective-permute-done | bytes 1048608 | tf_op jit(solution)/shard_map/ppermute | solution.py:326
  1223.2 4.7 collective-permute-start.1
  1227.8 100.4 %all_gather.47 = bf16[1024,256]{1,0:T(8,128)(2,1)S(1)} all-gather(bf16[256,256]{1,0:T(8,128)(2,1)S(1)} %pad_maximum_fusion.5), channel_id=1, replica_groups=mesh['shard'=2,'ctx'=4,'tp'=4] {'tp'}, dimensions={0}, use_global_device_ids=true | all-gather | bytes 655360 | tf_op jit(solution)/shard_map/all_gather | solution.py:124
  1328.5 2.4 convolution_bitcast_fusion.1
  1337.1 24.4 %all-gather.27.cloned.1.call-done = bf16[1024,2176]{1,0:T(8,128)(2,1)} async-done(((bf16[256,2176]{1,0:T(8,128)(2,1)}), bf16[1024,2176]{1,0:T(8,128)(2,1)}) %all-gather.27.cloned.1.call-update) | async-done | bytes 4456464 | tf_op jit(solution)/shard_map/all_gather | solution.py:124
  1362.6 4.0 convolution_bitcast_fusion
  1368.4 5.7 slice.65
  1374.1 2.6 slice.70
  1376.7 108.6 %all-reduce.3.cloned.1.call-done = (f32[8,2048,16]{1,2,0:T(8,128)}, f32[8,16,3,512]{3,2,1,0:T(4,128)}, f32[8,512,16]{1,2,0:T(8,128)}, f32[8,16,2048]{2,1,0:T(8,1...) async-done(((f32[8,2048,16]{1,2,0:T(8,128)}, f32[8,16,3,512]{3,2,1,0:T(4,128)}, ...) | async-done | bytes 7340048 | tf_op jit(solution)/shard_map/psum | solution.py:339
  1485.3 2.5 copy.96
  1487.8 2.4 copy.122
  (239 shorter events, 70.1 us)
Async XLA Ops:
  7.2 390.0 %copy-start = (bf16[8,16,2048]{2,1,0:T(8,128)(2,1)S(1)}, bf16[8,16,2048]{2,1,0:T(8,128)(2,1)}, u32[]{:S(2)}) copy-start(bf16[8,16,2048]{2,1,0:T(8,128)(2,1)} %param.37) | copy-start | bytes 1572868
  7.2 5.6 copy-start.44
  7.2 24.4 %all-gather.11.cloned.1.call-start = ((), (), s32[]{:S(2)}) async-start(), calls=%async_computation.7 | async-start | bytes 9437184 | tf_op jit(solution)/shard_map/all_gather | solution.py:200
  12.0 103.2 %all-gather.17.cloned.1.call-start = ((), (), s32[]{:S(2)}) async-start(), calls=%async_computation.10 | async-start | bytes 5242880 | tf_op jit(solution)/shard_map/all_gather | solution.py:177
  12.8 155.9 %all-gather.13.cloned.1.call-start = ((), (), s32[]{:S(2)}) async-start(), calls=%async_computation.8 | async-start | bytes 5242880 | tf_op jit(solution)/shard_map/all_gather | solution.py:216
  12.8 3.8 copy-start.3
  13.3 28.4 %copy-start.21 = (bf16[16,8,3,512]{3,1,2,0:T(8,128)(2,1)}, bf16[16,8,3,512]{3,1,2,0:T(8,128)(2,1)S(1)}, u32[]{:S(2)}) copy-start(bf16[16,8,3,512]{3,1,2,0:T(8,128)(2,1)S(1)} %copy.105) | copy-start | bytes 1179652
  13.4 4.5 copy-start.47
  13.4 4.5 copy-start.52
  17.9 3.8 copy-start.27
  23.0 18.7 %copy-start.23 = (bf16[1024,128]{1,0:T(8,128)(2,1)}, bf16[1024,128]{1,0:T(8,128)(2,1)S(1)}, u32[]{:S(2)}) copy-start(bf16[1024,128]{1,0:T(8,128)(2,1)S(1)} %fusion.21) | copy-start | bytes 786436
  44.0 179.4 %all-gather.15.cloned.1.call-start = ((), (), s32[]{:S(2)}) async-start(), calls=%async_computation.9 | async-start | bytes 5242880 | tf_op jit(solution)/shard_map/all_gather | solution.py:215
  45.3 245.2 %all-gather.19.cloned.1.call-start = ((), (), s32[]{:S(2)}) async-start(), calls=%async_computation.11 | async-start | bytes 12582912 | tf_op jit(solution)/shard_map/all_gather | solution.py:176
  115.2 187.9 %all-gather.25.cloned.1.call-start = ((), (), s32[]{:S(2)}) async-start(), calls=%async_computation.14 | async-start | bytes 12582912 | tf_op jit(solution)/shard_map/all_gather | solution.py:205
  115.8 202.4 %all-gather.23.cloned.1.call-start = ((), (), s32[]{:S(2)}) async-start(), calls=%async_computation.13 | async-start | bytes 12582912 | tf_op jit(solution)/shard_map/all_gather | solution.py:201
  123.6 99.8 %copy-start.16 = (bf16[4,256,4,128]{1,3,2,0:T(8,128)(2,1)}, bf16[4,256,4,128]{1,3,2,0:T(8,128)(2,1)S(1)}, u32[]{:S(2)}) copy-start(bf16[4,256,4,128]{1,3,2,0:T(8,128)(2,1)S(1)} %copy.88) | copy-start | bytes 3145732
  223.4 14.3 copy-start.4
  249.5 40.5 %all-to-all-start = ((bf16[4,256,512]{1,2,0:T(8,128)(2,1)}), bf16[4,256,512]{1,2,0:T(8,128)(2,1)S(1)}, u32[]{:S(2)}, u32[]{:S(2)}) async-start(bf16[4,256,512]{1,2,0:T(8,128)(2,1)} %bitcast.12), calls=%async_computation | async-start | bytes 2097152 | tf_op jit(solution)/shard_map/all_to_all | solution.py:235
  254.1 126.2 %all-gather.21.cloned.1.call-start = ((), (), s32[]{:S(2)}) async-start(), calls=%async_computation.12 | async-start | bytes 5242880 | tf_op jit(solution)/shard_map/all_gather | solution.py:124
  254.1 8.5 copy-start.45
  290.1 6.9 copy-start.19
  290.6 6.5 copy-start.41
  290.6 6.5 copy-start.30
  299.4 281.0 %reduce-scatter.8.cloned.1.call-start = ((), (), s32[]{:S(2)}) async-start(), calls=%async_computation.17 | async-start | bytes 11141120 | tf_op jit(solution)/shard_map/reduce_scatter | solution.py:116
  380.4 15.5 %copy-start.8 = (bf16[1024,2048]{1,0:T(8,128)(2,1)S(1)}, bf16[1024,2048]{1,0:T(8,128)(2,1)}, u32[]{:S(2)}) copy-start(bf16[1024,2048]{1,0:T(8,128)(2,1)} %all-gather.21.cloned.1.call-done) | copy-start | bytes 12582916
  380.4 15.5 %copy-start.25 = (bf16[8,2048,16]{1,2,0:T(8,128)(2,1)S(1)}, bf16[8,2048,16]{1,2,0:T(8,128)(2,1)}, u32[]{:S(2)}) copy-start(bf16[8,2048,16]{1,2,0:T(8,128)(2,1)} %param.36) | copy-start | bytes 1572868
  397.1 7.0 copy-start.32
  397.1 7.0 copy-start.43
  397.2 18.6 %slice-start.4 = ((s8[8388608]{0:T(1024)(128)(4,1)}), s8[4194304]{0:T(1024)(128)(4,1)S(1)}, s32[]{:S(2)}) async-start(s8[8388608]{0:T(1024)(128)(4,1)} %bitcast.221), calls=%async_computation.27 | async-start | bytes 8388608
  404.1 11.7 slice-start.5
  428.9 152.5 %copy-start.26 = (bf16[8,2048,16]{1,2,0:T(8,128)(2,1)S(1)}, bf16[8,2048,16]{1,2,0:T(8,128)(2,1)}, u32[]{:S(2)}) copy-start(bf16[8,2048,16]{1,2,0:T(8,128)(2,1)} %param.36) | copy-start | bytes 1572868
  428.9 301.6 %reduce-scatter.10.cloned.1.call-start = ((), (), s32[]{:S(2)}) async-start(), calls=%async_computation.18 | async-start | bytes 10485760 | tf_op jit(solution)/shard_map/reduce_scatter | solution.py:303
  581.4 6.5 slice-start
  583.7 3.7 copy-start.31
  583.8 4.2 slice-start.1
  587.4 2.9 copy-start.18
  627.6 12.5 copy-start.17
  636.8 3.3 copy-start.2
  645.0 174.9 %reduce-scatter.12.cloned.1.call-start = ((), (), s32[]{:S(2)}) async-start(), calls=%async_computation.19 | async-start | bytes 10485760 | tf_op jit(solution)/shard_map/reduce_scatter | solution.py:304
  656.7 318.4 %reduce-scatter.6.cloned.1.call-start = ((), (), s32[]{:S(2)}) async-start(), calls=%async_computation.15 | async-start | bytes 11141120 | tf_op jit(solution)/shard_map/reduce_scatter | solution.py:116
  656.9 3.9 copy-start.10
  676.4 454.8 %reduce-scatter.14.cloned.1.call-start = ((), (), s32[]{:S(2)}) async-start(), calls=%async_computation.20 | async-start | bytes 11141120 | tf_op jit(solution)/shard_map/reduce_scatter | solution.py:116
  735.5 94.5 %copy-start.22 = (bf16[16,8,3,512]{3,1,2,0:T(8,128)(2,1)S(1)}, bf16[16,8,3,512]{3,1,2,0:T(8,128)(2,1)}, u32[]{:S(2)}) copy-start(bf16[16,8,3,512]{3,1,2,0:T(8,128)(2,1)} %copy-done.21) | copy-start | bytes 1179652
  830.1 3.0 copy-start.6
  846.1 286.0 %copy-start.28 = (bf16[8,2048,16]{1,2,0:T(8,128)(2,1)S(1)}, bf16[8,2048,16]{1,2,0:T(8,128)(2,1)}, u32[]{:S(2)}) copy-start(bf16[8,2048,16]{1,2,0:T(8,128)(2,1)} %param.32) | copy-start | bytes 1572868
  846.1 286.0 %copy-start.48 = (f32[2048]{0:T(1024)S(1)}, f32[2048]{0:T(1024)}, u32[]{:S(2)}) copy-start(f32[2048]{0:T(1024)} %param.24) | copy-start | bytes 24580
  846.1 489.8 %all-gather.29.cloned.1.call-start = ((), (), s32[]{:S(2)}) async-start(), calls=%async_computation.21 | async-start | bytes 5570560 | tf_op jit(solution)/shard_map/all_gather | solution.py:124
  1137.6 3.0 copy-start.29
  1140.5 221.0 %all-gather.27.cloned.1.call-start = ((), (), s32[]{:S(2)}) async-start(), calls=%async_computation.16 | async-start | bytes 5570560 | tf_op jit(solution)/shard_map/all_gather | solution.py:124
  1140.6 3.2 copy-start.42
  1143.7 5.8 copy-start.33
  1143.8 341.5 %all-reduce.3.cloned.1.call-start = ((), (), s32[]{:S(2)}) async-start(), calls=%async_computation.22 | async-start | bytes 15204352 | tf_op jit(solution)/shard_map/psum | solution.py:339
  1145.4 76.4 %collective-permute-start = (f32[128,2048]{1,0:T(8,128)S(1)}, f32[128,2048]{1,0:T(8,128)}, u32[]{:S(2)}, u32[]{:S(2)}) collective-permute-start(f32[128,2048]{1,0:T(8,128)S(1)} %fusion.51), channel_id=1, source_target_pairs={{0,1},{1,0},{2,3},{3,2},{4,5},{5,4},{6,7},{7,6},{8,9},{9,8},{10,11... | collective-permute-start | bytes 3145736 | tf_op jit(solution)/shard_map/ppermute | solution.py:326
  1149.6 4.4 copy-start.11
  1223.2 109.5 %collective-permute-start.1 = (f32[128,2048]{1,0:T(8,128)S(1)}, f32[128,2048]{1,0:T(8,128)S(1)}, u32[]{:S(2)}, u32[]{:S(2)}) collective-permute-start(f32[128,2048]{1,0:T(8,128)S(1)} %add.215), channel_id=1, source_target_pairs={{0,2},{1,3},{2,0},{3,1},{4,6},{5,7},{6,4},{7,5},{8,10},{9,11},{10,... | collective-permute-start | bytes 3145736 | tf_op jit(solution)/shard_map/ppermute | solution.py:326
  1362.6 4.0 copy-start.5
  1368.4 5.7 slice-start.2
  1368.4 5.7 slice-start.3
  1485.3 6.6 copy-start.38
  1485.3 7.5 copy-start.37
  1485.3 8.5 copy-start.36
  1487.8 7.0 copy-start.35
  1491.8 3.9 copy-start.34
  1491.8 4.9 copy-start.1
  (16 other events, 30.9 us)
Sparse Core Ops, SparseCore 0:
  12.1 19.4 all-gather.10
  33.2 81.9 all-gather.16
  117.6 51.0 all-gather.12
  170.9 52.4 all-gather.14
  224.8 19.8 all-gather.18
  246.1 21.0 all-gather.24
  268.7 21.0 all-gather.22
  299.5 80.7 all-gather.20
  429.0 151.3 reduce-scatter.7
  645.1 85.3 reduce-scatter.9
  733.6 86.3 reduce-scatter.11
  822.1 152.8 reduce-scatter.5
  977.4 153.6 reduce-scatter.13
  1140.7 116.5 all-gather.28
  1258.6 102.8 all-gather.26
  1368.5 116.7 all-reduce.2
